TPU v7x, 32 devices: a whole 2x2x4 slice. The times are simulated.
32 devices in a mesh: seq: 8 (over z, core), exp: 4 (over y, x).
Axes of the slice: x: 2, y: 2, z: 4, core: 2. Of those that a mesh axis runs over, the one named last changes fastest.
Arguments:
- queries: bfloat16 [768, 4096], P('seq', 'exp'), may hold values from -17 to 17
- keys: bfloat16 [768, 1024], P('seq', 'exp'), may hold values from -17 to 17
- values: bfloat16 [768, 1024], P('seq', 'exp'), may hold values from -6 to 6
- residual: bfloat16 [768, 4096], P('seq', 'exp'), may hold values from -48 to 48
- norm_gain: float32 [4096], P('exp'), may hold values from 0.1 to 1.9
- routes: int32 [768, 2], P('seq'), may hold values from 0 to 3, all different within a row; in each aligned block of 96 rows (0 to 95, 96 to 191, ...) at most 72 rows name the same one
- gates: float32 [768, 2], P('seq'), may hold values from 0.1 to 0.9
- w_gate: bfloat16 [4, 4096, 14336], P('exp', None, 'seq'), may hold values from -0.09375 to 0.09375
- w_up: bfloat16 [4, 4096, 14336], P('exp', None, 'seq'), may hold values from -0.09375 to 0.09375
- w_down: bfloat16 [4, 14336, 4096], P('exp', 'seq'), may hold values from -0.046875 to 0.046875
Outputs:
- attended: bfloat16 [768, 4096], P('seq', 'exp')
- layer_out: bfloat16 [768, 4096], P('seq', 'exp')
Inputs may be any that keep to these rules, and one draw needn't show every extreme that they name: `routes`: each row names 2 different experts. In the rows of one device no expert is named more than 72 times, a bound that some block reaches.
All inputs are finite; a program needn't handle non-finite values.
Results may differ from a plain program's by a relative error of at most 0.0075.
Values may be sent and summed in bfloat16 or wider, within the bound.
No kernel may reach another device: no remote copies, remote signals or barrier semaphores. Data moves between devices by JAX's collectives and lax.ppermute only.
A program may use at most 128 MiB of HBM per device.

v0:
```python
import math

import jax
import jax.numpy as jnp
from jax import lax
from jax.sharding import PartitionSpec as P

D = 4096
QUERY_HEADS = 32
KEY_VALUE_HEADS = 8
HEAD_WIDTH = 128
TOP = 2


def shards(queries, keys, values, residual, norm_gain, routes, gates, w_gate, w_up, w_down):
    tok_rows = queries.shape[0]
    local_width = queries.shape[1]
    local_heads = keys.shape[1] // HEAD_WIDTH
    group_width = QUERY_HEADS // KEY_VALUE_HEADS
    exp_count = lax.axis_size("exp")
    score_scale = 1.0 / math.sqrt(HEAD_WIDTH)
    first_pos = lax.axis_index("seq") * tok_rows
    query_pos = first_pos + jnp.arange(tok_rows, dtype=jnp.int32)
    query_grouped = queries.reshape(tok_rows, local_heads, group_width, HEAD_WIDTH)
    running_max = jnp.full((local_heads, group_width, tok_rows), -1e30, jnp.float32)
    key_block = lax.all_gather(keys, "seq", axis=0, tiled=True)
    value_block = lax.all_gather(values, "seq", axis=0, tiled=True)
    length = key_block.shape[0]
    key_piece = key_block.reshape(length, local_heads, HEAD_WIDTH)
    value_piece = value_block.reshape(length, local_heads, HEAD_WIDTH)
    scores = (
        jnp.einsum("tkgd,pkd->kgtp", query_grouped, key_piece, preferred_element_type=jnp.float32)
        * score_scale
    )
    key_pos = jnp.arange(length, dtype=jnp.int32)
    causal_mask = key_pos[None, :] <= query_pos[:, None]
    scores = jnp.where(causal_mask, scores, -1e30)
    new_max = jnp.maximum(running_max, jnp.max(scores, axis=-1))
    exp_terms = jnp.where(causal_mask, jnp.exp(scores - new_max[..., None]), 0.0)
    new_sum = jnp.sum(exp_terms, axis=-1)
    new_weighted = jnp.einsum(
        "kgtp,pkd->kgtd",
        exp_terms.astype(jnp.bfloat16),
        value_piece,
        preferred_element_type=jnp.float32,
    )
    attn = new_weighted / new_sum[..., None]
    attn = jnp.transpose(attn, (2, 0, 1, 3)).reshape(tok_rows, local_width)
    attended = (residual.astype(jnp.float32) + attn).astype(jnp.bfloat16)
    stream = attended.astype(jnp.float32)
    square_total = lax.psum(jnp.sum(stream * stream, axis=1), "exp")
    normed = (stream * lax.rsqrt(square_total[:, None] / D + 1e-05) * norm_gain[None, :]).astype(
        jnp.bfloat16
    )
    experts = exp_count * w_gate.shape[0]
    capacity = min(tok_rows, 3 * TOP * tok_rows // (2 * experts))
    expert_ids = routes.reshape(tok_rows * TOP)
    one_hot = (expert_ids[:, None] == jnp.arange(experts, dtype=jnp.int32)[None, :]).astype(
        jnp.int32
    )
    before = jnp.cumsum(one_hot, axis=0) - one_hot
    slot_index = jnp.sum(before * one_hot, axis=1)
    dest_slot = expert_ids * capacity + slot_index
    slot_match = (
        dest_slot[:, None] == jnp.arange(experts * capacity, dtype=jnp.int32)[None, :]
    ).astype(jnp.float32)
    dispatch = jnp.sum(jnp.transpose(slot_match).reshape(experts * capacity, tok_rows, TOP), axis=2)
    outgoing = jnp.dot(
        dispatch.astype(jnp.bfloat16), normed, preferred_element_type=jnp.float32
    ).astype(jnp.bfloat16)
    outgoing = outgoing.reshape(experts, capacity, local_width)
    gate_mat = w_gate[0]
    up_mat = w_up[0]
    down_mat = w_down[0]
    arrived = lax.all_to_all(outgoing, "exp", split_axis=0, concat_axis=2, tiled=True)
    local_rows = arrived.reshape(capacity, D)
    flat_rows = lax.all_gather(local_rows, "seq", axis=0, tiled=True)
    hidden = (
        jax.nn.silu(jnp.dot(flat_rows, gate_mat, preferred_element_type=jnp.float32))
        * jnp.dot(flat_rows, up_mat, preferred_element_type=jnp.float32)
    ).astype(jnp.bfloat16)
    summed = lax.psum_scatter(
        jnp.dot(hidden, down_mat, preferred_element_type=jnp.float32).astype(jnp.bfloat16),
        "seq",
        scatter_dimension=0,
        tiled=True,
    )
    expert_out = summed.reshape(1, capacity, exp_count, local_width)
    returned = lax.all_to_all(expert_out, "exp", split_axis=2, concat_axis=0, tiled=True)
    returned_rows = returned.reshape(experts * capacity, local_width)
    weighted_match = slot_match * gates.reshape(tok_rows * TOP)[:, None]
    mixing = jnp.sum(weighted_match.reshape(tok_rows, TOP, experts * capacity), axis=1)
    expert_mix = jnp.dot(mixing, returned_rows.astype(jnp.float32), precision=lax.Precision.HIGHEST)
    layer_out = (stream + expert_mix).astype(jnp.bfloat16)
    return (attended, layer_out)


def solution(mesh):
    in_specs = (
        P("seq", "exp"),
        P("seq", "exp"),
        P("seq", "exp"),
        P("seq", "exp"),
        P("exp"),
        P("seq", None),
        P("seq", None),
        P("exp", None, "seq"),
        P("exp", None, "seq"),
        P("exp", "seq", None),
    )
    out_specs = (P("seq", "exp"), P("seq", "exp"))
    return jax.shard_map(shards, mesh=mesh, in_specs=in_specs, out_specs=out_specs, check_vma=False)
```

profile of v0, /device:TPU:0, one launch (start us, length us, event | category | flops | bytes accessed | tf_op | source)
XLA Modules:
  0.0 239.6 jit_solution(2482209283824322313)
XLA Ops:
  7.2 0.0 copy-start.3
  7.2 0.0 all-gather.2.cloned.1.call-start
  7.2 0.1 iota_compare_fusion.2
  7.4 16.4 %all_gather.9 = bf16[768,256]{1,0:T(8,128)(2,1)S(1)} all-gather(bf16[96,256]{1,0:T(8,128)(2,1)} %param.11), channel_id=1, replica_groups=mesh['seq'=8,'exp'=4] {'seq'}, dimensions={0}, use_global_device_ids=true | all-gather | bytes 442368 | tf_op jit(solution)/shard_map/all_gather | solution.py:26
  23.8 0.2 copy.61
  24.0 1.0 reshape.89
  25.0 0.6 fusion.13
  25.7 0.0 copy-done.3
  25.7 14.4 %all_gather.10 = bf16[768,256]{1,0:T(8,128)(2,1)S(1)} all-gather(bf16[96,256]{1,0:T(8,128)(2,1)S(1)} %copy-done.3), channel_id=1, replica_groups=mesh['seq'=8,'exp'=4] {'seq'}, dimensions={0}, use_global_device_ids=true | all-gather | bytes 442368 | tf_op jit(solution)/shard_map/all_gather | solution.py:27
  40.1 0.2 copy.64
  40.3 0.8 fusion.15
  41.1 0.0 copy-start.2
  41.1 0.0 copy-start.7
  41.1 0.0 copy-start.6
  41.1 0.8 fusion.17
  41.9 0.3 copy.66
  42.2 0.2 reshape.91
  42.4 0.0 copy-done.2
  42.4 0.2 fusion.24
  42.5 0.0 copy-start
  42.5 9.9 %psum.7 = f32[96]{0:T(128)S(1)} all-reduce(f32[96]{0:T(128)S(1)} %get-tuple-element.2), channel_id=1, replica_groups=mesh['seq'=8,'exp'=4] {'exp'}, use_global_device_ids=true, to_apply=%region_8.9 | all-reduce | flops 96 | bytes 768 | tf_op jit(solution)/shard_map/psum | solution.py:51
  52.4 0.0 copy-done.7
  52.4 0.1 copy.67
  52.5 0.1 eq.44
  52.7 1.2 reduce-window.6
  54.0 0.1 slice.12
  54.0 0.1 copy.68
  54.2 0.1 copy.69
  54.3 0.1 add_bitcast_fusion
  54.4 0.1 reduce_sum.49
  54.5 0.1 copy.70
  54.6 0.0 copy-start.4
  54.6 0.1 convert_reduce_fusion
  54.7 0.5 copy-done.4
  55.2 0.0 copy-done.6
  55.2 0.4 convolution_convert_fusion
  55.6 10.6 %all_to_all.30 = bf16[4,72,1024]{2,1,0:T(8,128)(2,1)S(1)} all-to-all(bf16[4,72,1024]{2,1,0:T(8,128)(2,1)S(1)} %bitcast.71), channel_id=1, replica_groups=mesh['seq'=8,'exp'=4] {'exp'}, dimensions={0} | all-to-all | bytes 1179648 | tf_op jit(solution)/shard_map/all_to_all | solution.py:75
  66.1 0.5 copy.71
  66.6 1.0 copy.80
  67.6 0.0 all-gather.2.cloned.1.call-update
  67.6 0.2 reduce-scatter.2.cloned.1.call-start
  67.9 50.6 %all-gather.2.cloned.1.call-done = bf16[576,4096]{1,0:T(8,128)(2,1)} async-done(((bf16[72,4096]{1,0:T(8,128)(2,1)}), bf16[576,4096]{1,0:T(8,128)(2,1)}) %all-gather.2.cloned.1.call-update) | async-done | bytes 4718608 | tf_op jit(solution)/shard_map/all_gather | solution.py:77
  118.5 14.7 %fusion.4 = f32[576,1792]{1,0:T(8,128)} fusion(bf16[576,4096]{1,0:T(8,128)(2,1)} %all-gather.2.cloned.1.call-done, bf16[1,4096,1792]{2,1,0:T(8,128)(2,1)} %param.17), kind=kOutput, calls=%fused_computation.4 | convolution fusion | flops 8455716864 | bytes 23527424 | tf_op jit(solution)/shard_map/dot_general | solution.py:79
  133.2 0.0 copy-done
  133.2 30.9 %fusion.6 = bf16[576,4096]{1,0:T(8,128)(2,1)} fusion(bf16[1,1792,4096]{2,1,0:T(8,128)(2,1)} %param.19, f32[576,1792]{1,0:T(8,128)} %fusion.4, bf16[576,4096]{1,0:T(8,128)(2,1)} %all-gather.2.cloned.1.call-done, bf16[1,4096,1792]{2,1,0:T(8,128)(2,1)} %param.18), kind=kOutput, calls=%fused_computation.6 | convolution fusion | flops 16919986176 | bytes 42926080 | tf_op jit(solution)/shard_map/dot_general | solution.py:83
  164.0 0.0 copy-start.5
  164.0 0.0 copy-start.8
  164.1 0.0 copy-start.1
  164.1 0.0 reduce-scatter.2.cloned.1.call-update
  164.1 53.8 %reduce-scatter.2.cloned.1.call-done = bf16[72,4096]{1,0:T(8,128)(2,1)} async-done(((bf16[576,4096]{1,0:T(8,128)(2,1)}), bf16[72,4096]{1,0:T(8,128)(2,1)}) %reduce-scatter.2.cloned.1.call-update) | async-done | bytes 589840 | tf_op jit(solution)/shard_map/reduce_scatter | solution.py:82
  217.9 2.0 reshape.96
  219.9 1.0 copy.72
  220.9 3.6 %all-to-all-start.1 = ((bf16[1,72,4,1024]{3,1,0,2:T(8,128)(2,1)}), bf16[1,72,4,1024]{3,1,0,2:T(8,128)(2,1)S(1)}, u32[]{:S(2)}, u32[]{:S(2)}) async-start(bf16[1,72,4,1024]{3,1,0,2:T(8,128)(2,1)} %copy.72), calls=%async_computation.2 | async-start | bytes 1179648 | tf_op jit(solution)/shard_map/all_to_all | solution.py:89
  224.5 0.0 copy-done.5
  224.5 0.0 copy-done.8
  224.5 0.1 select_reduce_fusion
  224.6 6.8 %all-to-all-done.1 = bf16[1,72,4,1024]{3,1,0,2:T(8,128)(2,1)S(1)} async-done(((bf16[1,72,4,1024]{3,1,0,2:T(8,128)(2,1)}), bf16[1,72,4,1024]{3,1,0,2:T(8,128)(2,1)S(1)}, u32[]{:S(2)}, u32[]{:S(2)}) %all-to-all-start.1) | async-done | bytes 589856 | tf_op jit(solution)/shard_map/all_to_all | solution.py:89
  231.5 0.0 copy-done.1
  231.5 1.2 fusion.23
  (11 shorter events, 0.1 us)
Async XLA Ops:
  7.2 18.5 %copy-start.3 = (bf16[96,256]{1,0:T(8,128)(2,1)S(1)}, bf16[96,256]{1,0:T(8,128)(2,1)}, u32[]{:S(2)}) copy-start(bf16[96,256]{1,0:T(8,128)(2,1)} %param.12) | copy-start | bytes 147460
  7.2 111.3 %all-gather.2.cloned.1.call-start = ((), (), s32[]{:S(2)}) async-start(), calls=%async_computation.3 | async-start | bytes 5308416 | tf_op jit(solution)/shard_map/all_gather | solution.py:77
  41.1 1.3 copy-start.2
  41.1 11.4 %copy-start.7 = (s32[96,2]{0,1:T(2,128)S(1)}, s32[96,2]{0,1:T(2,128)}, u32[]{:S(2)}) copy-start(s32[96,2]{0,1:T(2,128)} %param.15) | copy-start | bytes 2308
  41.1 14.1 %copy-start.6 = (f32[1024]{0:T(1024)S(1)}, f32[1024]{0:T(1024)}, u32[]{:S(2)}) copy-start(f32[1024]{0:T(1024)} %param.14) | copy-start | bytes 12292
  42.5 90.7 %copy-start = (bf16[96,1024]{1,0:T(8,128)(2,1)}, bf16[96,1024]{1,0:T(8,128)(2,1)S(1)}, u32[]{:S(2)}) copy-start(bf16[96,1024]{1,0:T(8,128)(2,1)S(1)} %get-tuple-element.3) | copy-start | bytes 589828
  54.6 0.6 copy-start.4
  67.6 150.2 %reduce-scatter.2.cloned.1.call-start = ((), (), s32[]{:S(2)}) async-start(), calls=%async_computation.4 | async-start | bytes 5308416 | tf_op jit(solution)/shard_map/reduce_scatter | solution.py:82
  164.0 60.5 %copy-start.5 = (s32[96,2]{0,1:T(2,128)S(1)}, s32[96,2]{0,1:T(2,128)}, u32[]{:S(2)}) copy-start(s32[96,2]{0,1:T(2,128)} %copy-done.4) | copy-start | bytes 2308
  164.0 60.5 %copy-start.8 = (f32[96,2]{0,1:T(2,128)S(1)}, f32[96,2]{0,1:T(2,128)}, u32[]{:S(2)}) copy-start(f32[96,2]{0,1:T(2,128)} %param.16) | copy-start | bytes 2308
  164.1 67.4 %copy-start.1 = (bf16[96,1024]{1,0:T(8,128)(2,1)S(1)}, bf16[96,1024]{1,0:T(8,128)(2,1)}, u32[]{:S(2)}) copy-start(bf16[96,1024]{1,0:T(8,128)(2,1)} %copy-done) | copy-start | bytes 589828
  220.9 10.6 %all-to-all-start.1 = ((bf16[1,72,4,1024]{3,1,0,2:T(8,128)(2,1)}), bf16[1,72,4,1024]{3,1,0,2:T(8,128)(2,1)S(1)}, u32[]{:S(2)}, u32[]{:S(2)}) async-start(bf16[1,72,4,1024]{3,1,0,2:T(8,128)(2,1)} %copy.72), calls=%async_computation.2 | async-start | bytes 1179648 | tf_op jit(solution)/shard_map/all_to_all | solution.py:89
Sparse Core Ops, SparseCore 0:
  67.8 50.6 all-gather.1
  164.2 53.6 reduce-scatter.1
where the time goes:
time: 240 us
  waiting for transfers between devices  111 us (46%)
  blocking collectives  51.3 us (21%)
  matrix products  48.6 us (20%)
  between operations  14.2 us (6%)
  local copies, waits for them, and re-layouts  7.56 us (3%)
  starting transfers between devices  3.9 us (2%)
  other arithmetic  2.62 us (1%)
    reduce_scatter x1, waiting for transfers between devices, shards(): lax.psum_scatter(jnp.dot(hidden, down_mat, preferred_element_type=jnp.flo...  53.8 us
    all_gather x1, waiting for transfers between devices, shards(): flat_rows = lax.all_gather(local_rows, 'seq', axis=0, tiled=True)  50.6 us
    dot_general x1, matrix products, shards(): jnp.dot(hidden, down_mat, preferred_element_type=jnp.float32)  30.9 us
    all_gather x1, blocking collectives, shards(): key_block = lax.all_gather(keys, 'seq', axis=0, tiled=True)  16.4 us
    dot_general x1, matrix products, shards(): jnp.dot(flat_rows, gate_mat, preferred_element_type=jnp.float32)  14.7 us
    all_gather x1, blocking collectives, shards(): value_block = lax.all_gather(values, 'seq', axis=0, tiled=True)  14.4 us
    all_to_all x1, blocking collectives, shards(): lax.all_to_all(outgoing, 'exp', split_axis=0, concat_axis=2, tiled=True)  10.6 us
    psum x1, blocking collectives, shards(): square_total = lax.psum(jnp.sum(stream * stream, axis=1), 'exp')  9.92 us
  transfers between devices with their start and end apart: 3, of which 3 were waited for; matrix products, arithmetic and copies ran while one was open for 0% of the time, Pallas kernels for 0%

commit v1 on v0

v1 whole, which is shorter than its diff:
```python
import math

import jax
import jax.numpy as jnp
from jax import lax
from jax.experimental import pallas as pl
from jax.experimental.pallas import tpu as pltpu
from jax.sharding import PartitionSpec as P

D = 4096
QUERY_HEADS = 32
KEY_VALUE_HEADS = 8
HEAD_WIDTH = 128
TOP = 2
CHUNKS = 2


def chip_shift(x, step):
    n = lax.axis_size("seq")
    return lax.ppermute(x, "seq", [(i, (i + 2 * step) % n) for i in range(n)])


def core_swap(x):
    n = lax.axis_size("seq")
    return lax.ppermute(x, "seq", [(i, i ^ 1) for i in range(n)])


def exp_swap(x, k):
    n = lax.axis_size("exp")
    return lax.ppermute(x, "exp", [(i, i ^ k) for i in range(n)])


def low_half(rows):
    return (rows // 2 + 7) // 8 * 8


def gather_seq(x):
    chips = lax.axis_size("seq") // 2
    far = chips // 2
    cut = low_half(x.shape[0])
    blocks = [None] * chips
    blocks[0] = x
    ahead = behind = x
    for d in range(1, far):
        behind = chip_shift(behind, 1)
        ahead = chip_shift(ahead, -1)
        blocks[-d] = behind
        blocks[d] = ahead
    top = chip_shift(behind[:cut], 1)
    bottom = chip_shift(ahead[cut:], -1)
    blocks[far] = jnp.concatenate([top, bottom], axis=0)
    mine = jnp.concatenate(blocks, axis=0)
    other = core_swap(mine)
    return jnp.concatenate([mine, other], axis=0)


def add(a, b):
    return (a.astype(jnp.float32) + b.astype(jnp.float32)).astype(a.dtype)


def reduce_seq(partial):
    n = lax.axis_size("seq")
    chips = n // 2
    far = chips // 2
    half = partial.shape[0] // 2
    rows = half // chips
    cut = low_half(rows)
    other = core_swap(partial[half:])
    both = add(partial[:half], other)
    block = [both[d * rows : (d + 1) * rows] for d in range(chips)]
    top = chip_shift(block[far][:cut], 1)
    bottom = chip_shift(block[far][cut:], -1)
    for d in range(far - 1, 0, -1):
        if d == far - 1:
            up = jnp.concatenate([add(block[d][:cut], top), block[d][cut:]], axis=0)
            down = jnp.concatenate([block[-d][:cut], add(block[-d][cut:], bottom)], axis=0)
        else:
            up = add(block[d], up)
            down = add(block[-d], down)
        up = chip_shift(up, 1)
        down = chip_shift(down, -1)
    f32 = jnp.float32
    return (block[0].astype(f32) + up.astype(f32) + down.astype(f32)).astype(partial.dtype)


def ordered(pieces, me):
    bit = 1
    while bit < len(pieces):
        flag = (me & bit) != 0
        pieces = [jnp.where(flag, pieces[p ^ bit], pieces[p]) for p in range(len(pieces))]
        bit *= 2
    return pieces


def hidden_body(rows, gate_mat, up_mat, out):
    x = rows[...]
    g = jnp.dot(x, gate_mat[0], preferred_element_type=jnp.float32)
    u = jnp.dot(x, up_mat[0], preferred_element_type=jnp.float32)
    out[...] = (g / (1.0 + jnp.exp(-g)) * u).astype(out.dtype)


def hidden_units(flat, w_gate, w_up, first, count, width):
    rows, depth = flat.shape
    weight = pl.BlockSpec((1, depth, width), lambda j: (0, 0, j + first))
    return pl.pallas_call(
        hidden_body,
        grid=(count,),
        in_specs=[pl.BlockSpec((rows, depth), lambda j: (0, 0)), weight, weight],
        out_specs=pl.BlockSpec((rows, width), lambda j: (0, j)),
        out_shape=jax.ShapeDtypeStruct((rows, count * width), flat.dtype),
        cost_estimate=pl.CostEstimate(
            flops=4 * rows * depth * count * width,
            bytes_accessed=4 * depth * count * width,
            transcendentals=0,
        ),
        compiler_params=pltpu.CompilerParams(vmem_limit_bytes=40 << 20),
    )(flat, w_gate, w_up)


def down_body(*refs):
    hiddens, mat, out = refs[:-2], refs[-2], refs[-1]
    total = None
    at = 0
    for h in hiddens:
        part = jnp.dot(
            h[...], mat[0, at : at + h.shape[1], :], preferred_element_type=jnp.float32
        )
        total = part if total is None else total + part
        at += h.shape[1]
    out[...] = total.astype(out.dtype)


def down_product(hiddens, w_down):
    rows = hiddens[0].shape[0]
    _, units, depth = w_down.shape
    width = 512
    return pl.pallas_call(
        down_body,
        grid=(depth // width,),
        in_specs=[pl.BlockSpec(h.shape, lambda j: (0, 0)) for h in hiddens]
        + [pl.BlockSpec((1, units, width), lambda j: (0, 0, j))],
        out_specs=pl.BlockSpec((rows, width), lambda j: (0, j)),
        out_shape=jax.ShapeDtypeStruct((rows, depth), hiddens[0].dtype),
        cost_estimate=pl.CostEstimate(
            flops=2 * rows * depth * units, bytes_accessed=2 * depth * units, transcendentals=0
        ),
        compiler_params=pltpu.CompilerParams(vmem_limit_bytes=40 << 20),
    )(*hiddens, w_down)


def expert(flat, w_gate, w_up, w_down):
    units = w_gate.shape[2]
    width = 256 if units % 256 == 0 else units
    count = units // width
    split = [(0, count // 2), (count // 2, count - count // 2)] if count > 1 else [(0, 1)]
    hiddens = [hidden_units(flat, w_gate, w_up, first, n, width) for first, n in split]
    return down_product(hiddens, w_down)


def attend(queries, keys, values):
    tok_rows, local_width = queries.shape
    kv_width = keys.shape[1]
    local_heads = kv_width // HEAD_WIDTH
    group_width = QUERY_HEADS // KEY_VALUE_HEADS
    score_scale = 1.0 / math.sqrt(HEAD_WIDTH)
    first_pos = lax.axis_index("seq") * tok_rows
    query_pos = first_pos + jnp.arange(tok_rows, dtype=jnp.int32)
    query_grouped = queries.reshape(tok_rows, local_heads, group_width, HEAD_WIDTH)
    both = lax.all_gather(jnp.concatenate([keys, values], axis=1), "seq", axis=0, tiled=True)
    length = both.shape[0]
    key_piece = both[:, :kv_width].reshape(length, local_heads, HEAD_WIDTH)
    value_piece = both[:, kv_width:].reshape(length, local_heads, HEAD_WIDTH)
    key_pos = jnp.arange(length, dtype=jnp.int32)
    scores = (
        jnp.einsum("tkgd,pkd->kgtp", query_grouped, key_piece, preferred_element_type=jnp.float32)
        * score_scale
    )
    causal_mask = key_pos[None, :] <= query_pos[:, None]
    scores = jnp.where(causal_mask, scores, -1e30)
    row_max = jnp.max(scores, axis=-1)
    exp_terms = jnp.where(causal_mask, jnp.exp(scores - row_max[..., None]), 0.0)
    row_sum = jnp.sum(exp_terms, axis=-1)
    weighted = jnp.einsum(
        "kgtp,pkd->kgtd",
        exp_terms.astype(jnp.bfloat16),
        value_piece,
        preferred_element_type=jnp.float32,
    )
    attn = weighted / row_sum[..., None]
    return jnp.transpose(attn, (2, 0, 1, 3)).reshape(tok_rows, local_width)


def shards(queries, keys, values, residual, norm_gain, routes, gates, w_gate, w_up, w_down):
    tok_rows, local_width = queries.shape
    exp_count = lax.axis_size("exp")
    me = lax.axis_index("exp")
    capacity = min(tok_rows, 3 * TOP * tok_rows // (2 * exp_count))
    gain = jnp.concatenate(
        ordered([norm_gain] + [exp_swap(norm_gain, k) for k in range(1, exp_count)], me)
    )
    expert_ids = routes.reshape(tok_rows * TOP)
    relative = expert_ids ^ me
    one_hot = (relative[:, None] == jnp.arange(exp_count, dtype=jnp.int32)[None, :])
    number = jnp.arange(tok_rows * TOP, dtype=jnp.int32)
    earlier = (number[None, :] < number[:, None]).astype(jnp.bfloat16)
    before = jnp.dot(earlier, one_hot.astype(jnp.bfloat16), preferred_element_type=jnp.float32)
    slot_index = jnp.sum(jnp.where(one_hot, before, 0.0), axis=1).astype(jnp.int32)
    dest_slot = (relative * capacity + slot_index).reshape(tok_rows, TOP)
    slots = jnp.arange(exp_count * capacity, dtype=jnp.int32)
    dispatch = jnp.zeros((exp_count * capacity, tok_rows), jnp.float32)
    mixing = jnp.zeros((tok_rows, exp_count * capacity), jnp.float32)
    for t in range(TOP):
        dispatch = dispatch + (slots[:, None] == dest_slot[None, :, t])
        mixing = mixing + jnp.where(dest_slot[:, t, None] == slots[None, :], gates[:, t, None], 0.0)

    attn = attend(queries, keys, values)
    attended = (residual.astype(jnp.float32) + attn).astype(jnp.bfloat16)
    outgoing = jnp.dot(
        dispatch.astype(jnp.bfloat16), attended, preferred_element_type=jnp.float32
    ).astype(jnp.bfloat16)
    pieces = [outgoing[:capacity]]
    for k in range(1, exp_count):
        pieces.append(exp_swap(outgoing[k * capacity : (k + 1) * capacity], k))
    rows = jnp.concatenate(ordered(pieces, me), axis=1).astype(jnp.float32)
    mean_square = jnp.sum(rows * rows, axis=1, keepdims=True) / D
    normed = (rows * lax.rsqrt(mean_square + 1e-05) * gain[None, :]).astype(jnp.bfloat16)

    step = (-(-capacity // CHUNKS) + 7) // 8 * 8
    returned = [[] for _ in range(exp_count)]
    for start in range(0, capacity, step):
        flat = gather_seq(normed[start : min(start + step, capacity)])
        partial = expert(flat, w_gate, w_up, w_down)
        summed = reduce_seq(partial)
        for k in range(exp_count):
            piece = lax.dynamic_slice_in_dim(summed, (me ^ k) * local_width, local_width, axis=1)
            returned[k].append(piece if k == 0 else exp_swap(piece, k))
    returned_rows = jnp.concatenate([piece for pieces in returned for piece in pieces], axis=0)
    expert_mix = jnp.dot(mixing, returned_rows.astype(jnp.float32), precision=lax.Precision.HIGHEST)
    layer_out = (attended.astype(jnp.float32) + expert_mix).astype(jnp.bfloat16)
    return (attended, layer_out)


def solution(mesh):
    in_specs = (
        P("seq", "exp"),
        P("seq", "exp"),
        P("seq", "exp"),
        P("seq", "exp"),
        P("exp"),
        P("seq", None),
        P("seq", None),
        P("exp", None, "seq"),
        P("exp", None, "seq"),
        P("exp", "seq", None),
    )
    out_specs = (P("seq", "exp"), P("seq", "exp"))

    return jax.shard_map(shards, mesh=mesh, in_specs=in_specs, out_specs=out_specs, check_vma=False)
```

time: 240 us -> 187 us (0.78)
  Pallas kernels: 0 us -> 52.8 us
  waiting for transfers between devices: 111 us -> 59.2 us
  matrix products: 48.6 us -> 4.23 us
  starting transfers between devices: 3.9 us -> 47.4 us
  blocking collectives: 51.3 us -> 16.1 us
  between operations: 14.2 us -> 1.22 us
  local copies, waits for them, and re-layouts: 7.56 us -> 2.58 us
    ppermute x0 -> x32, waiting for transfers between devices: none -> 59.2 us  [the longest x16 48.6 us: chip_shift(): return lax.ppermute(x, 'seq', [(i, (i + 2 * step) % n) for i in range(n)])]
    reduce_scatter x1 -> x0, waiting for transfers between devices: 53.8 us -> none  [shards(): lax.psum_scatter(jnp.dot(hidden, down_mat, preferred_element_type=jnp.flo...]
    pallas_call x0 -> x6, Pallas kernels: none -> 52.8 us  [the longest x4 32.9 us: hidden_units(): pl.pallas_call(hidden_body, grid=(count,), in_specs=[pl.BlockSpec((rows,...]
    all_gather x1 -> x0, waiting for transfers between devices: 50.6 us -> none  [shards(): flat_rows = lax.all_gather(local_rows, 'seq', axis=0, tiled=True)]
    ppermute x0 -> x32, starting transfers between devices: none -> 47.4 us  [the longest x16 31.2 us: chip_shift(): return lax.ppermute(x, 'seq', [(i, (i + 2 * step) % n) for i in range(n)])]
    dot_general x5 -> x4, matrix products: 47.4 us -> 1.78 us  [the longest x1 0.87 us: attend(): jnp.einsum('kgtp,pkd->kgtd', exp_terms.astype(jnp.bfloat16), value_piece,...]
    all_gather x2 -> x1, blocking collectives: 30.9 us -> 16.1 us  [attend(): lax.all_gather(jnp.concatenate([keys, values], axis=1), 'seq', axis=0, ti...]
    all_to_all x1 -> x0, blocking collectives: 10.6 us -> none  [shards(): lax.all_to_all(outgoing, 'exp', split_axis=0, concat_axis=2, tiled=True)]
  transfers between devices with their start and end apart: 3 -> 32, of which waited for: 3 -> 17; matrix products, arithmetic and copies ran while one was open for 0% -> 4% of each run, Pallas kernels for 0% -> 28%
where the time goes in v1:
time: 187 us; the launch traced here: 186 us
  waiting for transfers between devices  59.2 us (32%)
  Pallas kernels  52.8 us (28%)
  starting transfers between devices  47.4 us (25%)
  blocking collectives  16.1 us (9%)
  matrix products  4.23 us (2%)
  other arithmetic  2.68 us (1%)
  local copies, waits for them, and re-layouts  2.58 us (1%)
    ppermute x16, waiting for transfers between devices, chip_shift(): return lax.ppermute(x, 'seq', [(i, (i + 2 * step) % n) for i in range(n)])  48.6 us
    pallas_call x4, Pallas kernels, hidden_units(): pl.pallas_call(hidden_body, grid=(count,), in_specs=[pl.BlockSpec((rows,...  32.9 us
    ppermute x16, starting transfers between devices, chip_shift(): return lax.ppermute(x, 'seq', [(i, (i + 2 * step) % n) for i in range(n)])  31.2 us
    pallas_call x2, Pallas kernels, down_product(): pl.pallas_call(down_body, grid=(depth // width,), in_specs=[pl.BlockSpec(...  20 us
    all_gather x1, blocking collectives, attend(): lax.all_gather(jnp.concatenate([keys, values], axis=1), 'seq', axis=0, ti...  16.1 us
    ppermute x12, starting transfers between devices, exp_swap(): return lax.ppermute(x, 'exp', [(i, i ^ k) for i in range(n)])  15.4 us
    ppermute x12, waiting for transfers between devices, exp_swap(): return lax.ppermute(x, 'exp', [(i, i ^ k) for i in range(n)])  9.9 us
  transfers between devices with their start and end apart: 32, of which 17 were waited for; matrix products, arithmetic and copies ran while one was open for 4% of the time, Pallas kernels for 28%

profile of v1, /device:TPU:0, one launch (start us, length us, event | category | flops | bytes accessed | tf_op | source)
XLA Modules:
  0.0 186.2 jit_solution(17439182928689511854)
XLA Ops:
  0.6 4.0 %collective-permute-start.3 = (f32[1024]{0:T(1024)}, f32[1024]{0:T(1024)S(1)}, u32[]{:S(2)}, u32[]{:S(2)}) collective-permute-start(f32[1024]{0:T(1024)} %param.14), channel_id=1, source_target_pairs={{0,3},{1,2},{2,1},{3,0},{4,7},{5,6},{6,5},{7,4},{8,11},{9,10},{10,... | collective-permute-start | bytes 12296 | tf_op jit(solution)/shard_map/ppermute | solution.py:30
  4.6 0.5 collective-permute-start.4
  5.3 0.9 pad_maximum_fusion.5
  6.1 16.1 %all_gather.3 = bf16[768,512]{1,0:T(8,128)(2,1)S(1)} all-gather(bf16[96,512]{1,0:T(8,128)(2,1)S(1)} %pad_maximum_fusion.5), channel_id=1, replica_groups=mesh['seq'=8,'exp'=4] {'seq'}, dimensions={0}, use_global_device_ids=true | all-gather | bytes 884736 | tf_op jit(solution)/shard_map/all_gather | solution.py:169
  22.3 0.2 copy.41
  22.5 0.2 copy.40
  22.9 0.5 fusion.16
  23.4 1.1 fusion.43
  24.5 0.9 fusion.2
  25.4 0.3 copy.32
  25.7 0.2 reshape.47
  26.1 0.2 fusion.11
  26.3 0.1 convert_element_type.126
  26.5 0.2 slice_reduce_fusion.1
  26.8 0.3 convolution_convert_fusion
  27.1 2.5 %collective-permute-start = (bf16[72,1024]{1,0:T(8,128)(2,1)S(1)}, bf16[72,1024]{1,0:T(8,128)(2,1)S(1)}, u32[]{:S(2)}, u32[]{:S(2)}) collective-permute-start(bf16[72,1024]{1,0:T(8,128)(2,1)S(1)} %get-tuple-element.28), channel_id=1, source_target_pairs={{0,3},{1,2},{2,1},{3,0},{4,7},{5,6},{6,5},{7,4},{8,11},{9,10},{10,... | collective-permute-start | bytes 442376 | tf_op jit(solution)/shard_map/ppermute | solution.py:30
  29.6 0.5 collective-permute-start.1
  30.1 0.6 collective-permute-start.2
  30.8 4.0 %collective-permute-done = bf16[72,1024]{1,0:T(8,128)(2,1)S(1)} collective-permute-done((bf16[72,1024]{1,0:T(8,128)(2,1)S(1)}, bf16[72,1024]{1,0:T(8,128)(2,1)S(1)}, u32[]{:S(2)}, u32[]{:S(2)}) %collective-permute-start) | collective-permute-done | bytes 147488 | tf_op jit(solution)/shard_map/ppermute | solution.py:30
  34.8 2.5 %collective-permute-done.1 = bf16[72,1024]{1,0:T(8,128)(2,1)S(1)} collective-permute-done((bf16[72,1024]{1,0:T(8,128)(2,1)S(1)}, bf16[72,1024]{1,0:T(8,128)(2,1)S(1)}, u32[]{:S(2)}, u32[]{:S(2)}) %collective-permute-start.1) | collective-permute-done | bytes 147488 | tf_op jit(solution)/shard_map/ppermute | solution.py:30
  37.5 0.2 fusion.3
  37.7 0.2 fusion.5
  38.0 3.6 %collective-permute-start.16 = (bf16[32,4096]{1,0:T(8,128)(2,1)S(1)}, bf16[32,4096]{1,0:T(8,128)(2,1)S(1)}, u32[]{:S(2)}, u32[]{:S(2)}) collective-permute-start(bf16[32,4096]{1,0:T(8,128)(2,1)S(1)} %get-tuple-element.22), channel_id=1, source_target_pairs={{0,24},{4,28},{8,0},{12,4},{16,8},{20,12},{24,16},{28,20},{1,25},{... | collective-permute-start | bytes 786440 | tf_op jit(solution)/shard_map/ppermute | solution.py:20
  41.7 3.9 %collective-permute-start.6 = (bf16[40,4096]{1,0:T(8,128)(2,1)S(1)}, bf16[40,4096]{1,0:T(8,128)(2,1)S(1)}, u32[]{:S(2)}, u32[]{:S(2)}) collective-permute-start(bf16[40,4096]{1,0:T(8,128)(2,1)S(1)} %get-tuple-element.25), channel_id=1, source_target_pairs={{0,24},{4,28},{8,0},{12,4},{16,8},{20,12},{24,16},{28,20},{1,25},{... | collective-permute-start | bytes 983048 | tf_op jit(solution)/shard_map/ppermute | solution.py:20
  45.6 8.8 %collective-permute-done.17 = bf16[32,4096]{1,0:T(8,128)(2,1)S(1)} collective-permute-done((bf16[32,4096]{1,0:T(8,128)(2,1)S(1)}, bf16[32,4096]{1,0:T(8,128)(2,1)S(1)}, u32[]{:S(2)}, u32[]{:S(2)}) %collective-permute-start.17) | collective-permute-done | bytes 262176 | tf_op jit(solution)/shard_map/ppermute | solution.py:20
  54.4 2.0 %collective-permute-start.18 = (bf16[16,4096]{1,0:T(8,128)(2,1)S(1)}, bf16[16,4096]{1,0:T(8,128)(2,1)S(1)}, u32[]{:S(2)}, u32[]{:S(2)}) collective-permute-start(bf16[16,4096]{1,0:T(8,128)(2,1)S(1)} %slice.177), channel_id=1, source_target_pairs={{0,8},{4,12},{8,16},{12,20},{16,24},{20,28},{24,0},{28,4},{1,9},{5... | collective-permute-start | bytes 393224 | tf_op jit(solution)/shard_map/ppermute | solution.py:20
  56.5 1.9 %collective-permute-start.19 = (bf16[16,4096]{1,0:T(8,128)(2,1)S(1)}, bf16[16,4096]{1,0:T(8,128)(2,1)S(1)}, u32[]{:S(2)}, u32[]{:S(2)}) collective-permute-start(bf16[16,4096]{1,0:T(8,128)(2,1)S(1)} %slice.178), channel_id=1, source_target_pairs={{0,24},{4,28},{8,0},{12,4},{16,8},{20,12},{24,16},{28,20},{1,25},{... | collective-permute-start | bytes 393224 | tf_op jit(solution)/shard_map/ppermute | solution.py:20
  58.4 10.1 %collective-permute-done.7 = bf16[40,4096]{1,0:T(8,128)(2,1)S(1)} collective-permute-done((bf16[40,4096]{1,0:T(8,128)(2,1)S(1)}, bf16[40,4096]{1,0:T(8,128)(2,1)S(1)}, u32[]{:S(2)}, u32[]{:S(2)}) %collective-permute-start.7) | collective-permute-done | bytes 327712 | tf_op jit(solution)/shard_map/ppermute | solution.py:20
  68.6 2.0 %collective-permute-start.8 = (bf16[24,4096]{1,0:T(8,128)(2,1)S(1)}, bf16[24,4096]{1,0:T(8,128)(2,1)S(1)}, u32[]{:S(2)}, u32[]{:S(2)}) collective-permute-start(bf16[24,4096]{1,0:T(8,128)(2,1)S(1)} %slice.165), channel_id=1, source_target_pairs={{0,8},{4,12},{8,16},{12,20},{16,24},{20,28},{24,0},{28,4},{1,9},{5... | collective-permute-start | bytes 589832 | tf_op jit(solution)/shard_map/ppermute | solution.py:20
  70.6 2.1 %collective-permute-start.9 = (bf16[16,4096]{1,0:T(8,128)(2,1)S(1)}, bf16[16,4096]{1,0:T(8,128)(2,1)S(1)}, u32[]{:S(2)}, u32[]{:S(2)}) collective-permute-start(bf16[16,4096]{1,0:T(8,128)(2,1)S(1)} %slice.166), channel_id=1, source_target_pairs={{0,24},{4,28},{8,0},{12,4},{16,8},{20,12},{24,16},{28,20},{1,25},{... | collective-permute-start | bytes 393224 | tf_op jit(solution)/shard_map/ppermute | solution.py:20
  72.8 0.8 collective-permute-done.19
  73.8 4.6 %collective-permute-done.8 = bf16[24,4096]{1,0:T(8,128)(2,1)S(1)} collective-permute-done((bf16[24,4096]{1,0:T(8,128)(2,1)S(1)}, bf16[24,4096]{1,0:T(8,128)(2,1)S(1)}, u32[]{:S(2)}, u32[]{:S(2)}) %collective-permute-start.8) | collective-permute-done | bytes 196640 | tf_op jit(solution)/shard_map/ppermute | solution.py:20
  78.4 1.2 collective-permute-done.9
  79.9 7.1 %shard_map.116.refs_0_ = bf16[256,768]{1,0:T(8,128)(2,1)S(1)} custom-call(bf16[256,4096]{1,0:T(8,128)(2,1)S(1)} %constant_dynamic-update-slice_fusion.16.rows, bf16[1,4096,1792]{2,1,0:T(8,128)(2,1)} %gate_mat.7, bf16[1,4096,1792]{2,1,0:T(8,128)(2,1)} %up_mat.7), custom_call_target="tpu_custom_call" | custom-call | flops 3221225472 | bytes 12582912 | tf_op jit(solution)/shard_map/pallas_call | solution.py:105
  87.0 8.8 %shard_map.117.refs_1_ = bf16[256,1024]{1,0:T(8,128)(2,1)S(1)} custom-call(bf16[256,4096]{1,0:T(8,128)(2,1)S(1)} %constant_dynamic-update-slice_fusion.16.rows, bf16[1,4096,1792]{2,1,0:T(8,128)(2,1)} %gate_mat.7, bf16[1,4096,1792]{2,1,0:T(8,128)(2,1)} %up_mat.7), custom_call_target="tpu_custom_call" | custom-call | flops 4294967296 | bytes 16777216 | tf_op jit(solution)/shard_map/pallas_call | solution.py:105
  95.7 9.7 %shard_map.118 = bf16[256,4096]{1,0:T(8,128)(2,1)S(1)} custom-call(bf16[256,768]{1,0:T(8,128)(2,1)S(1)} %shard_map.116.refs_0_, bf16[256,1024]{1,0:T(8,128)(2,1)S(1)} %shard_map.117.refs_1_, bf16[1,1792,4096]{2,1,0:T(8,128)(2,1)} %refs_2_.3), custom_call_target="tpu_custom_call" | custom-call | flops 3758096384 | bytes 14680064 | tf_op jit(solution)/shard_map/pallas_call | solution.py:137
  105.5 0.6 collective-permute-start.21
  106.2 7.6 %shard_map.113.refs_0_ = bf16[320,768]{1,0:T(8,128)(2,1)S(1)} custom-call(bf16[320,4096]{1,0:T(8,128)(2,1)S(1)} %constant_dynamic-update-slice_fusion.5.rows, bf16[1,4096,1792]{2,1,0:T(8,128)(2,1)} %gate_mat.7, bf16[1,4096,1792]{2,1,0:T(8,128)(2,1)} %up_mat.7), custom_call_target="tpu_custom_call" | custom-call | flops 4026531840 | bytes 12582912 | tf_op jit(solution)/shard_map/pallas_call | solution.py:105
  113.8 9.4 %shard_map.114.refs_1_ = bf16[320,1024]{1,0:T(8,128)(2,1)S(1)} custom-call(bf16[320,4096]{1,0:T(8,128)(2,1)S(1)} %constant_dynamic-update-slice_fusion.5.rows, bf16[1,4096,1792]{2,1,0:T(8,128)(2,1)} %gate_mat.7, bf16[1,4096,1792]{2,1,0:T(8,128)(2,1)} %up_mat.7), custom_call_target="tpu_custom_call" | custom-call | flops 5368709120 | bytes 16777216 | tf_op jit(solution)/shard_map/pallas_call | solution.py:105
  123.3 0.2 add_convert_fusion.1
  123.6 0.8 collective-permute-start.22
  124.4 3.6 %collective-permute-start.24 = (bf16[16,4096]{1,0:T(8,128)(2,1)S(1)}, bf16[16,4096]{1,0:T(8,128)(2,1)S(1)}, u32[]{:S(2)}, u32[]{:S(2)}) collective-permute-start(bf16[16,4096]{1,0:T(8,128)(2,1)S(1)} %get-tuple-element.11), channel_id=1, source_target_pairs={{0,24},{4,28},{8,0},{12,4},{16,8},{20,12},{24,16},{28,20},{1,25},{... | collective-permute-start | bytes 393224 | tf_op jit(solution)/shard_map/ppermute | solution.py:20
  128.0 10.3 %shard_map.115 = bf16[320,4096]{1,0:T(8,128)(2,1)S(1)} custom-call(bf16[320,768]{1,0:T(8,128)(2,1)S(1)} %shard_map.113.refs_0_, bf16[320,1024]{1,0:T(8,128)(2,1)S(1)} %shard_map.114.refs_1_, bf16[1,1792,4096]{2,1,0:T(8,128)(2,1)} %refs_2_.3), custom_call_target="tpu_custom_call" | custom-call | flops 4697620480 | bytes 14680064 | tf_op jit(solution)/shard_map/pallas_call | solution.py:137
  138.6 2.0 %collective-permute-start.25 = (bf16[32,4096]{1,0:T(8,128)(2,1)S(1)}, bf16[32,4096]{1,0:T(8,128)(2,1)S(1)}, u32[]{:S(2)}, u32[]{:S(2)}) collective-permute-start(bf16[32,4096]{1,0:T(8,128)(2,1)S(1)} %pad_maximum_fusion.4), channel_id=1, source_target_pairs={{0,24},{4,28},{8,0},{12,4},{16,8},{20,12},{24,16},{28,20},{1,25},{... | collective-permute-start | bytes 786440 | tf_op jit(solution)/shard_map/ppermute | solution.py:20
  140.7 0.7 collective-permute-done.11
  141.5 0.4 add_convert_fusion
  141.9 3.1 %collective-permute-start.14 = (bf16[16,4096]{1,0:T(8,128)(2,1)S(1)}, bf16[16,4096]{1,0:T(8,128)(2,1)S(1)}, u32[]{:S(2)}, u32[]{:S(2)}) collective-permute-start(bf16[16,4096]{1,0:T(8,128)(2,1)S(1)} %get-tuple-element.7), channel_id=1, source_target_pairs={{0,24},{4,28},{8,0},{12,4},{16,8},{20,12},{24,16},{28,20},{1,25},{... | collective-permute-start | bytes 393224 | tf_op jit(solution)/shard_map/ppermute | solution.py:20
  145.1 10.7 %collective-permute-done.14 = bf16[16,4096]{1,0:T(8,128)(2,1)S(1)} collective-permute-done((bf16[16,4096]{1,0:T(8,128)(2,1)S(1)}, bf16[16,4096]{1,0:T(8,128)(2,1)S(1)}, u32[]{:S(2)}, u32[]{:S(2)}) %collective-permute-start.14) | collective-permute-done | bytes 131104 | tf_op jit(solution)/shard_map/ppermute | solution.py:20
  155.9 4.3 %collective-permute-start.15 = (bf16[40,4096]{1,0:T(8,128)(2,1)S(1)}, bf16[40,4096]{1,0:T(8,128)(2,1)S(1)}, u32[]{:S(2)}, u32[]{:S(2)}) collective-permute-start(bf16[40,4096]{1,0:T(8,128)(2,1)S(1)} %pad_maximum_fusion.2), channel_id=1, source_target_pairs={{0,24},{4,28},{8,0},{12,4},{16,8},{20,12},{24,16},{28,20},{1,25},{... | collective-permute-start | bytes 983048 | tf_op jit(solution)/shard_map/ppermute | solution.py:20
  160.2 0.2 collective-permute-done.12
  160.5 1.8 collective-permute-start.13
  162.3 6.5 %collective-permute-done.15 = bf16[40,4096]{1,0:T(8,128)(2,1)S(1)} collective-permute-done((bf16[40,4096]{1,0:T(8,128)(2,1)S(1)}, bf16[40,4096]{1,0:T(8,128)(2,1)S(1)}, u32[]{:S(2)}, u32[]{:S(2)}) %collective-permute-start.15) | collective-permute-done | bytes 327712 | tf_op jit(solution)/shard_map/ppermute | solution.py:20
  168.8 5.5 %collective-permute-done.13 = bf16[40,4096]{1,0:T(8,128)(2,1)S(1)} collective-permute-done((bf16[40,4096]{1,0:T(8,128)(2,1)S(1)}, bf16[40,4096]{1,0:T(8,128)(2,1)S(1)}, u32[]{:S(2)}, u32[]{:S(2)}) %collective-permute-start.13) | collective-permute-done | bytes 327712 | tf_op jit(solution)/shard_map/ppermute | solution.py:20
  174.5 1.6 collective-permute-start.26
  176.1 0.6 collective-permute-start.27
  176.7 1.5 collective-permute-start.28
  178.2 0.5 collective-permute-start.29
  178.7 1.0 collective-permute-start.30
  179.8 1.9 %collective-permute-start.31 = (bf16[32,1024]{1,0:T(8,128)(2,1)S(1)}, bf16[32,1024]{1,0:T(8,128)(2,1)S(1)}, u32[]{:S(2)}, u32[]{:S(2)}) collective-permute-start(bf16[32,1024]{1,0:T(8,128)(2,1)S(1)} %get-tuple-element.37), channel_id=1, source_target_pairs={{0,3},{1,2},{2,1},{3,0},{4,7},{5,6},{6,5},{7,4},{8,11},{9,10},{10,... | collective-permute-start | bytes 196616 | tf_op jit(solution)/shard_map/ppermute | solution.py:30
  181.7 0.8 collective-permute-done.28
  182.4 0.7 collective-permute-done.29
  183.1 0.9 collective-permute-done.30
  184.1 0.9 collective-permute-done.31
  184.9 1.3 fusion.10
  (90 shorter events, 2.9 us)
Async XLA Ops:
  0.6 29.5 %collective-permute-start.3 = (f32[1024]{0:T(1024)}, f32[1024]{0:T(1024)S(1)}, u32[]{:S(2)}, u32[]{:S(2)}) collective-permute-start(f32[1024]{0:T(1024)} %param.14), channel_id=1, source_target_pairs={{0,3},{1,2},{2,1},{3,0},{4,7},{5,6},{6,5},{7,4},{8,11},{9,10},{10,... | collective-permute-start | bytes 12296 | tf_op jit(solution)/shard_map/ppermute | solution.py:30
  4.6 26.1 %collective-permute-start.4 = (f32[1024]{0:T(1024)}, f32[1024]{0:T(1024)S(1)}, u32[]{:S(2)}, u32[]{:S(2)}) collective-permute-start(f32[1024]{0:T(1024)} %param.14), channel_id=1, source_target_pairs={{0,2},{1,3},{2,0},{3,1},{4,6},{5,7},{6,4},{7,5},{8,10},{9,11},{10,... | collective-permute-start | bytes 12296 | tf_op jit(solution)/shard_map/ppermute | solution.py:30
  5.1 25.6 %collective-permute-start.5 = (f32[1024]{0:T(1024)}, f32[1024]{0:T(1024)S(1)}, u32[]{:S(2)}, u32[]{:S(2)}) collective-permute-start(f32[1024]{0:T(1024)} %param.14), channel_id=1, source_target_pairs={{0,1},{1,0},{2,3},{3,2},{4,5},{5,4},{6,7},{7,6},{8,9},{9,8},{10,11... | collective-permute-start | bytes 12296 | tf_op jit(solution)/shard_map/ppermute | solution.py:30
  5.3 17.4 %copy-start.1 = (bf16[96,1024]{1,0:T(8,128)(2,1)S(1)}, bf16[96,1024]{1,0:T(8,128)(2,1)}, u32[]{:S(2)}) copy-start(bf16[96,1024]{1,0:T(8,128)(2,1)} %param.10) | copy-start | bytes 589828
  24.5 1.4 copy-start.4
  25.4 1.3 copy-start.2
  25.7 4.4 %copy-start.5 = (f32[96,2]{0,1:T(2,128)S(1)}, f32[96,2]{0,1:T(2,128)}, u32[]{:S(2)}) copy-start(f32[96,2]{0,1:T(2,128)} %param.16) | copy-start | bytes 2308
  25.7 5.0 %copy-start.3 = (f32[1024]{0:T(1024)S(1)}, f32[1024]{0:T(1024)}, u32[]{:S(2)}) copy-start(f32[1024]{0:T(1024)} %param.14) | copy-start | bytes 12292
  26.7 158.2 %copy-start = (bf16[96,1024]{1,0:T(8,128)(2,1)}, bf16[96,1024]{1,0:T(8,128)(2,1)S(1)}, u32[]{:S(2)}) copy-start(bf16[96,1024]{1,0:T(8,128)(2,1)S(1)} %add_convert_fusion.5) | copy-start | bytes 589828
  27.1 7.7 %collective-permute-start = (bf16[72,1024]{1,0:T(8,128)(2,1)S(1)}, bf16[72,1024]{1,0:T(8,128)(2,1)S(1)}, u32[]{:S(2)}, u32[]{:S(2)}) collective-permute-start(bf16[72,1024]{1,0:T(8,128)(2,1)S(1)} %get-tuple-element.28), channel_id=1, source_target_pairs={{0,3},{1,2},{2,1},{3,0},{4,7},{5,6},{6,5},{7,4},{8,11},{9,10},{10,... | collective-permute-start | bytes 442376 | tf_op jit(solution)/shard_map/ppermute | solution.py:30
  29.6 7.7 %collective-permute-start.1 = (bf16[72,1024]{1,0:T(8,128)(2,1)S(1)}, bf16[72,1024]{1,0:T(8,128)(2,1)S(1)}, u32[]{:S(2)}, u32[]{:S(2)}) collective-permute-start(bf16[72,1024]{1,0:T(8,128)(2,1)S(1)} %get-tuple-element.27), channel_id=1, source_target_pairs={{0,2},{1,3},{2,0},{3,1},{4,6},{5,7},{6,4},{7,5},{8,10},{9,11},{10,... | collective-permute-start | bytes 442376 | tf_op jit(solution)/shard_map/ppermute | solution.py:30
  30.1 7.3 %collective-permute-start.2 = (bf16[72,1024]{1,0:T(8,128)(2,1)S(1)}, bf16[72,1024]{1,0:T(8,128)(2,1)S(1)}, u32[]{:S(2)}, u32[]{:S(2)}) collective-permute-start(bf16[72,1024]{1,0:T(8,128)(2,1)S(1)} %get-tuple-element.26), channel_id=1, source_target_pairs={{0,1},{1,0},{2,3},{3,2},{4,5},{5,4},{6,7},{7,6},{8,9},{9,8},{10,11... | collective-permute-start | bytes 442376 | tf_op jit(solution)/shard_map/ppermute | solution.py:30
  38.0 18.4 %collective-permute-start.16 = (bf16[32,4096]{1,0:T(8,128)(2,1)S(1)}, bf16[32,4096]{1,0:T(8,128)(2,1)S(1)}, u32[]{:S(2)}, u32[]{:S(2)}) collective-permute-start(bf16[32,4096]{1,0:T(8,128)(2,1)S(1)} %get-tuple-element.22), channel_id=1, source_target_pairs={{0,24},{4,28},{8,0},{12,4},{16,8},{20,12},{24,16},{28,20},{1,25},{... | collective-permute-start | bytes 786440 | tf_op jit(solution)/shard_map/ppermute | solution.py:20
  41.6 12.8 %collective-permute-start.17 = (bf16[32,4096]{1,0:T(8,128)(2,1)S(1)}, bf16[32,4096]{1,0:T(8,128)(2,1)S(1)}, u32[]{:S(2)}, u32[]{:S(2)}) collective-permute-start(bf16[32,4096]{1,0:T(8,128)(2,1)S(1)} %get-tuple-element.22), channel_id=1, source_target_pairs={{0,8},{4,12},{8,16},{12,20},{16,24},{20,28},{24,0},{28,4},{1,9},{5... | collective-permute-start | bytes 786440 | tf_op jit(solution)/shard_map/ppermute | solution.py:20
  41.7 28.9 %collective-permute-start.6 = (bf16[40,4096]{1,0:T(8,128)(2,1)S(1)}, bf16[40,4096]{1,0:T(8,128)(2,1)S(1)}, u32[]{:S(2)}, u32[]{:S(2)}) collective-permute-start(bf16[40,4096]{1,0:T(8,128)(2,1)S(1)} %get-tuple-element.25), channel_id=1, source_target_pairs={{0,24},{4,28},{8,0},{12,4},{16,8},{20,12},{24,16},{28,20},{1,25},{... | collective-permute-start | bytes 983048 | tf_op jit(solution)/shard_map/ppermute | solution.py:20
  45.6 23.0 %collective-permute-start.7 = (bf16[40,4096]{1,0:T(8,128)(2,1)S(1)}, bf16[40,4096]{1,0:T(8,128)(2,1)S(1)}, u32[]{:S(2)}, u32[]{:S(2)}) collective-permute-start(bf16[40,4096]{1,0:T(8,128)(2,1)S(1)} %get-tuple-element.25), channel_id=1, source_target_pairs={{0,8},{4,12},{8,16},{12,20},{16,24},{20,28},{24,0},{28,4},{1,9},{5... | collective-permute-start | bytes 983048 | tf_op jit(solution)/shard_map/ppermute | solution.py:20
  54.4 18.3 %collective-permute-start.18 = (bf16[16,4096]{1,0:T(8,128)(2,1)S(1)}, bf16[16,4096]{1,0:T(8,128)(2,1)S(1)}, u32[]{:S(2)}, u32[]{:S(2)}) collective-permute-start(bf16[16,4096]{1,0:T(8,128)(2,1)S(1)} %slice.177), channel_id=1, source_target_pairs={{0,8},{4,12},{8,16},{12,20},{16,24},{20,28},{24,0},{28,4},{1,9},{5... | collective-permute-start | bytes 393224 | tf_op jit(solution)/shard_map/ppermute | solution.py:20
  56.5 17.1 %collective-permute-start.19 = (bf16[16,4096]{1,0:T(8,128)(2,1)S(1)}, bf16[16,4096]{1,0:T(8,128)(2,1)S(1)}, u32[]{:S(2)}, u32[]{:S(2)}) collective-permute-start(bf16[16,4096]{1,0:T(8,128)(2,1)S(1)} %slice.178), channel_id=1, source_target_pairs={{0,24},{4,28},{8,0},{12,4},{16,8},{20,12},{24,16},{28,20},{1,25},{... | collective-permute-start | bytes 393224 | tf_op jit(solution)/shard_map/ppermute | solution.py:20
  68.6 9.8 %collective-permute-start.8 = (bf16[24,4096]{1,0:T(8,128)(2,1)S(1)}, bf16[24,4096]{1,0:T(8,128)(2,1)S(1)}, u32[]{:S(2)}, u32[]{:S(2)}) collective-permute-start(bf16[24,4096]{1,0:T(8,128)(2,1)S(1)} %slice.165), channel_id=1, source_target_pairs={{0,8},{4,12},{8,16},{12,20},{16,24},{20,28},{24,0},{28,4},{1,9},{5... | collective-permute-start | bytes 589832 | tf_op jit(solution)/shard_map/ppermute | solution.py:20
  70.6 9.1 %collective-permute-start.9 = (bf16[16,4096]{1,0:T(8,128)(2,1)S(1)}, bf16[16,4096]{1,0:T(8,128)(2,1)S(1)}, u32[]{:S(2)}, u32[]{:S(2)}) collective-permute-start(bf16[16,4096]{1,0:T(8,128)(2,1)S(1)} %slice.166), channel_id=1, source_target_pairs={{0,24},{4,28},{8,0},{12,4},{16,8},{20,12},{24,16},{28,20},{1,25},{... | collective-permute-start | bytes 393224 | tf_op jit(solution)/shard_map/ppermute | solution.py:20
  73.7 6.1 %collective-permute-start.20 = (bf16[128,4096]{1,0:T(8,128)(2,1)S(1)}, bf16[128,4096]{1,0:T(8,128)(2,1)S(1)}, u32[]{:S(2)}, u32[]{:S(2)}) collective-permute-start(bf16[128,4096]{1,0:T(8,128)(2,1)S(1)} %get-tuple-element.41), channel_id=1, source_target_pairs={{0,4},{4,0},{8,12},{12,8},{16,20},{20,16},{24,28},{28,24},{1,5},{5... | collective-permute-start | bytes 3145736 | tf_op jit(solution)/shard_map/ppermute | solution.py:25
  79.7 26.4 %collective-permute-start.10 = (bf16[160,4096]{1,0:T(8,128)(2,1)S(1)}, bf16[160,4096]{1,0:T(8,128)(2,1)S(1)}, u32[]{:S(2)}, u32[]{:S(2)}) collective-permute-start(bf16[160,4096]{1,0:T(8,128)(2,1)S(1)} %get-tuple-element.33), channel_id=1, source_target_pairs={{0,4},{4,0},{8,12},{12,8},{16,20},{20,16},{24,28},{28,24},{1,5},{5... | collective-permute-start | bytes 3932168 | tf_op jit(solution)/shard_map/ppermute | solution.py:25
  105.5 17.7 %collective-permute-start.21 = (bf16[128,4096]{1,0:T(8,128)(2,1)S(1)}, bf16[128,4096]{1,0:T(8,128)(2,1)S(1)}, u32[]{:S(2)}, u32[]{:S(2)}) collective-permute-start(bf16[128,4096]{1,0:T(8,128)(2,1)S(1)} %slice.180), channel_id=1, source_target_pairs={{0,4},{4,0},{8,12},{12,8},{16,20},{20,16},{24,28},{28,24},{1,5},{5... | collective-permute-start | bytes 3145736 | tf_op jit(solution)/shard_map/ppermute | solution.py:25
  123.6 14.9 %collective-permute-start.22 = (bf16[16,4096]{1,0:T(8,128)(2,1)S(1)}, bf16[16,4096]{1,0:T(8,128)(2,1)S(1)}, u32[]{:S(2)}, u32[]{:S(2)}) collective-permute-start(bf16[16,4096]{1,0:T(8,128)(2,1)S(1)} %get-tuple-element.10), channel_id=1, source_target_pairs={{0,8},{4,12},{8,16},{12,20},{16,24},{20,28},{24,0},{28,4},{1,9},{5... | collective-permute-start | bytes 393224 | tf_op jit(solution)/shard_map/ppermute | solution.py:20
  124.4 14.1 %collective-permute-start.24 = (bf16[16,4096]{1,0:T(8,128)(2,1)S(1)}, bf16[16,4096]{1,0:T(8,128)(2,1)S(1)}, u32[]{:S(2)}, u32[]{:S(2)}) collective-permute-start(bf16[16,4096]{1,0:T(8,128)(2,1)S(1)} %get-tuple-element.11), channel_id=1, source_target_pairs={{0,24},{4,28},{8,0},{12,4},{16,8},{20,12},{24,16},{28,20},{1,25},{... | collective-permute-start | bytes 393224 | tf_op jit(solution)/shard_map/ppermute | solution.py:20
  138.4 3.1 %collective-permute-start.11 = (bf16[160,4096]{1,0:T(8,128)(2,1)S(1)}, bf16[160,4096]{1,0:T(8,128)(2,1)S(1)}, u32[]{:S(2)}, u32[]{:S(2)}) collective-permute-start(bf16[160,4096]{1,0:T(8,128)(2,1)S(1)} %slice.168), channel_id=1, source_target_pairs={{0,4},{4,0},{8,12},{12,8},{16,20},{20,16},{24,28},{28,24},{1,5},{5... | collective-permute-start | bytes 3932168 | tf_op jit(solution)/shard_map/ppermute | solution.py:25
  138.6 23.6 %collective-permute-start.25 = (bf16[32,4096]{1,0:T(8,128)(2,1)S(1)}, bf16[32,4096]{1,0:T(8,128)(2,1)S(1)}, u32[]{:S(2)}, u32[]{:S(2)}) collective-permute-start(bf16[32,4096]{1,0:T(8,128)(2,1)S(1)} %pad_maximum_fusion.4), channel_id=1, source_target_pairs={{0,24},{4,28},{8,0},{12,4},{16,8},{20,12},{24,16},{28,20},{1,25},{... | collective-permute-start | bytes 786440 | tf_op jit(solution)/shard_map/ppermute | solution.py:20
  140.6 21.6 %collective-permute-start.23 = (bf16[32,4096]{1,0:T(8,128)(2,1)S(1)}, bf16[32,4096]{1,0:T(8,128)(2,1)S(1)}, u32[]{:S(2)}, u32[]{:S(2)}) collective-permute-start(bf16[32,4096]{1,0:T(8,128)(2,1)S(1)} %pad_maximum_fusion.3), channel_id=1, source_target_pairs={{0,8},{4,12},{8,16},{12,20},{16,24},{20,28},{24,0},{28,4},{1,9},{5... | collective-permute-start | bytes 786440 | tf_op jit(solution)/shard_map/ppermute | solution.py:20
  141.9 13.9 %collective-permute-start.14 = (bf16[16,4096]{1,0:T(8,128)(2,1)S(1)}, bf16[16,4096]{1,0:T(8,128)(2,1)S(1)}, u32[]{:S(2)}, u32[]{:S(2)}) collective-permute-start(bf16[16,4096]{1,0:T(8,128)(2,1)S(1)} %get-tuple-element.7), channel_id=1, source_target_pairs={{0,24},{4,28},{8,0},{12,4},{16,8},{20,12},{24,16},{28,20},{1,25},{... | collective-permute-start | bytes 393224 | tf_op jit(solution)/shard_map/ppermute | solution.py:20
  145.0 15.4 %collective-permute-start.12 = (bf16[24,4096]{1,0:T(8,128)(2,1)S(1)}, bf16[24,4096]{1,0:T(8,128)(2,1)S(1)}, u32[]{:S(2)}, u32[]{:S(2)}) collective-permute-start(bf16[24,4096]{1,0:T(8,128)(2,1)S(1)} %get-tuple-element.4), channel_id=1, source_target_pairs={{0,8},{4,12},{8,16},{12,20},{16,24},{20,28},{24,0},{28,4},{1,9},{5... | collective-permute-start | bytes 589832 | tf_op jit(solution)/shard_map/ppermute | solution.py:20
  155.9 12.9 %collective-permute-start.15 = (bf16[40,4096]{1,0:T(8,128)(2,1)S(1)}, bf16[40,4096]{1,0:T(8,128)(2,1)S(1)}, u32[]{:S(2)}, u32[]{:S(2)}) collective-permute-start(bf16[40,4096]{1,0:T(8,128)(2,1)S(1)} %pad_maximum_fusion.2), channel_id=1, source_target_pairs={{0,24},{4,28},{8,0},{12,4},{16,8},{20,12},{24,16},{28,20},{1,25},{... | collective-permute-start | bytes 983048 | tf_op jit(solution)/shard_map/ppermute | solution.py:20
  160.5 13.9 %collective-permute-start.13 = (bf16[40,4096]{1,0:T(8,128)(2,1)S(1)}, bf16[40,4096]{1,0:T(8,128)(2,1)S(1)}, u32[]{:S(2)}, u32[]{:S(2)}) collective-permute-start(bf16[40,4096]{1,0:T(8,128)(2,1)S(1)} %pad_maximum_fusion.1), channel_id=1, source_target_pairs={{0,8},{4,12},{8,16},{12,20},{16,24},{20,28},{24,0},{28,4},{1,9},{5... | collective-permute-start | bytes 983048 | tf_op jit(solution)/shard_map/ppermute | solution.py:20
  174.5 5.3 %collective-permute-start.26 = (bf16[40,1024]{1,0:T(8,128)(2,1)S(1)}, bf16[40,1024]{1,0:T(8,128)(2,1)S(1)}, u32[]{:S(2)}, u32[]{:S(2)}) collective-permute-start(bf16[40,1024]{1,0:T(8,128)(2,1)S(1)} %get-tuple-element.31), channel_id=1, source_target_pairs={{0,1},{1,0},{2,3},{3,2},{4,5},{5,4},{6,7},{7,6},{8,9},{9,8},{10,11... | collective-permute-start | bytes 245768 | tf_op jit(solution)/shard_map/ppermute | solution.py:30
  176.1 5.6 %collective-permute-start.27 = (bf16[32,1024]{1,0:T(8,128)(2,1)S(1)}, bf16[32,1024]{1,0:T(8,128)(2,1)S(1)}, u32[]{:S(2)}, u32[]{:S(2)}) collective-permute-start(bf16[32,1024]{1,0:T(8,128)(2,1)S(1)} %get-tuple-element.39), channel_id=1, source_target_pairs={{0,1},{1,0},{2,3},{3,2},{4,5},{5,4},{6,7},{7,6},{8,9},{9,8},{10,11... | collective-permute-start | bytes 196616 | tf_op jit(solution)/shard_map/ppermute | solution.py:30
  176.7 5.7 %collective-permute-start.28 = (bf16[40,1024]{1,0:T(8,128)(2,1)S(1)}, bf16[40,1024]{1,0:T(8,128)(2,1)S(1)}, u32[]{:S(2)}, u32[]{:S(2)}) collective-permute-start(bf16[40,1024]{1,0:T(8,128)(2,1)S(1)} %get-tuple-element.30), channel_id=1, source_target_pairs={{0,2},{1,3},{2,0},{3,1},{4,6},{5,7},{6,4},{7,5},{8,10},{9,11},{10,... | collective-permute-start | bytes 245768 | tf_op jit(solution)/shard_map/ppermute | solution.py:30
  178.2 4.9 %collective-permute-start.29 = (bf16[32,1024]{1,0:T(8,128)(2,1)S(1)}, bf16[32,1024]{1,0:T(8,128)(2,1)S(1)}, u32[]{:S(2)}, u32[]{:S(2)}) collective-permute-start(bf16[32,1024]{1,0:T(8,128)(2,1)S(1)} %get-tuple-element.38), channel_id=1, source_target_pairs={{0,2},{1,3},{2,0},{3,1},{4,6},{5,7},{6,4},{7,5},{8,10},{9,11},{10,... | collective-permute-start | bytes 196616 | tf_op jit(solution)/shard_map/ppermute | solution.py:30
  178.7 5.3 %collective-permute-start.30 = (bf16[40,1024]{1,0:T(8,128)(2,1)S(1)}, bf16[40,1024]{1,0:T(8,128)(2,1)S(1)}, u32[]{:S(2)}, u32[]{:S(2)}) collective-permute-start(bf16[40,1024]{1,0:T(8,128)(2,1)S(1)} %get-tuple-element.29), channel_id=1, source_target_pairs={{0,3},{1,2},{2,1},{3,0},{4,7},{5,6},{6,5},{7,4},{8,11},{9,10},{10,... | collective-permute-start | bytes 245768 | tf_op jit(solution)/shard_map/ppermute | solution.py:30
  179.8 5.2 %collective-permute-start.31 = (bf16[32,1024]{1,0:T(8,128)(2,1)S(1)}, bf16[32,1024]{1,0:T(8,128)(2,1)S(1)}, u32[]{:S(2)}, u32[]{:S(2)}) collective-permute-start(bf16[32,1024]{1,0:T(8,128)(2,1)S(1)} %get-tuple-element.37), channel_id=1, source_target_pairs={{0,3},{1,2},{2,1},{3,0},{4,7},{5,6},{6,5},{7,4},{8,11},{9,10},{10,... | collective-permute-start | bytes 196616 | tf_op jit(solution)/shard_map/ppermute | solution.py:30
